TPU v7x, 16 devices: a 4x2x1 block of a 4x4x4 slice. The times are simulated.
16 devices in a mesh: dp: 4 (over y, z, core), tp: 4 (over x).
Axes of the slice: x: 4, y: 2, z: 1, core: 2. Of those that a mesh axis runs over, the one named last changes fastest.
The devices are a block of a 4x4x4 slice.
Arguments:
- x: bfloat16 [256, 5120], P('dp'), parts along dimension 0
- k_cache: bfloat16 [256, 2048, 8, 160], P('dp', None, 'tp'), parts along dimension 0
- v_cache: bfloat16 [256, 2048, 8, 160], P('dp', None, 'tp'), parts along dimension 0
- gain_a: bfloat16 [5120], replicated
- wq: bfloat16 [5120, 5120], P(None, 'tp')
- wo: bfloat16 [5120, 5120], P('tp')
- gain_m: bfloat16 [5120], replicated
- w_gate: bfloat16 [5120, 13824], P(None, 'tp')
- w_up: bfloat16 [5120, 13824], P(None, 'tp')
- w_down: bfloat16 [13824, 5120], P('tp')
Outputs:
- output: bfloat16 [256, 5120], P('dp'), parts along dimension 0
There are 4 independent parts. A program takes and returns all parts, laid end to end along the dimension named above; an argument that names none is the same for every part.
All inputs are finite; a program needn't handle non-finite values.
Results may differ from a plain program's by a relative error of at most 0.017.
Values are sent between devices in bfloat16 or wider.
A program may use at most 1.5 GiB of HBM per device.

v0:
```python
import jax
import jax.numpy as jnp
from jax import lax
from jax.sharding import PartitionSpec as P

HEAD = 160
THETA = 10000


def normed(x, gain):
    wide = x.astype(jnp.float32)
    scale = lax.rsqrt(jnp.mean(wide * wide, -1, keepdims=True) + 1e-6)
    return (wide * scale * gain.astype(jnp.float32)).astype(jnp.bfloat16)


def turned(t, place, theta):
    half = t.shape[-1] // 2
    angle = place.astype(jnp.float32)[:, None] * theta ** (-jnp.arange(half, dtype=jnp.float32) / half)
    cos, sin = jnp.cos(angle)[:, None], jnp.sin(angle)[:, None]
    a, b = t[..., :half].astype(jnp.float32), t[..., half:].astype(jnp.float32)
    return jnp.concatenate([a * cos - b * sin, b * cos + a * sin], -1).astype(jnp.bfloat16)


def matmul(a, w):
    return jnp.dot(a, w, preferred_element_type=jnp.float32).astype(jnp.bfloat16)


def einsum(form, a, b):
    return jnp.einsum(form, a.astype(jnp.float32), b.astype(jnp.float32))


def seen_by(a, wq, k_cache, v_cache, head, theta):
    batch, cache, kv_heads = k_cache.shape[:3]
    place = jnp.full((batch,), cache - 1)
    q = turned(matmul(a, wq).reshape(batch, -1, head), place, theta).reshape(batch, kv_heads, -1, head)
    scores = einsum("bgsd,bugd->bgsu", q, k_cache) * head**-0.5
    weights = jax.nn.softmax(scores, -1).astype(jnp.bfloat16)
    return einsum("bgsu,bugd->bgsd", weights, v_cache).astype(jnp.bfloat16).reshape(batch, -1)


def hidden_of(b, w_gate, w_up):
    gate = jnp.dot(b, w_gate, preferred_element_type=jnp.float32)
    up = jnp.dot(b, w_up, preferred_element_type=jnp.float32)
    return (jax.nn.silu(gate) * up).astype(jnp.bfloat16)


def solution(mesh):
    def added(t, term):
        return (t.astype(jnp.float32) + lax.psum(term.astype(jnp.bfloat16), "tp").astype(jnp.float32)).astype(jnp.bfloat16)

    def step(x, k_cache, v_cache, gain_a, wq, wo, gain_m, w_gate, w_up, w_down):
        seen = seen_by(normed(x, gain_a), wq, k_cache, v_cache, HEAD, THETA)
        h = added(x, jnp.dot(seen, wo, preferred_element_type=jnp.float32))
        return added(h, jnp.dot(hidden_of(normed(h, gain_m), w_gate, w_up), w_down, preferred_element_type=jnp.float32))

    states, cache, columns, rows_of = P("dp", None), P("dp", None, "tp", None), P(None, "tp"), P("tp", None)
    return jax.shard_map(
        step,
        mesh=mesh,
        in_specs=(states, cache, cache, P(None), columns, rows_of, P(None), columns, columns, rows_of),
        out_specs=states,
        check_vma=False,
    )
```

profile of v0, /device:TPU:112, one launch (start us, length us, event | category | flops | bytes accessed | tf_op | source)
XLA Modules:
  0.0 212.8 jit_solution(484431851786123948)
XLA Ops:
  6.5 0.0 all-reduce.3.cloned.1.call-start
  6.6 0.7 convert_element_type.63
  7.3 1.3 fusion.6
  8.6 7.4 %convolution_convert_fusion.2 = bf16[64,1280]{1,0:T(8,128)(2,1)S(1)} fusion(bf16[5120,1280]{1,0:T(8,128)(2,1)} %param.14, bf16[64,5120]{1,0:T(8,128)(2,1)} %param.10, f32[5120]{0:T(1024)S(1)} %convert_element_type.63, f32[64]{0:T(128)S(1)} %add_rsqrt_fusion.1), kind=kOutput, calls=%fused_computation.9 | convolution fusion | flops 840253440 | bytes 13947136 | tf_op jit(solution)/shard_map/dot_general | solution.py:25
  16.1 0.3 reshape.39
  16.4 0.1 fusion.25
  16.5 30.2 %fusion.42 = (f32[64,2,4]{2,1,0:T(2,128)S(1)}, f32[64,2,4,2048]{3,2,1,0:T(4,128)}) fusion(bf16[64,2048,2,160]{1,3,2,0:T(8,128)(2,1)} %param.11, bf16[64,2,4,80]{3,2,1,0:T(4,128)(2,1)S(1)} %bitcast.11, bf16[64,2,4,80]{3,2,1,0:T(4,128)(2,1)S(1)} %bitcast.10), kind=kOutput, calls=%fused_computation.57 | convolution fusion | flops 339019776 | bytes 88246272 | tf_op jit(solution)/shard_map/sub | solution.py:37
  46.8 31.9 %fusion.14 = bf16[64,2,4,160]{3,2,1,0:T(4,128)(2,1)S(1)} fusion(bf16[64,2048,2,160]{1,3,2,0:T(8,128)(2,1)} %param.12, f32[64,2,4,2048]{3,2,1,0:T(4,128)} %get-tuple-element.10, f32[64,2,4]{2,1,0:T(2,128)S(1)} %get-tuple-element.9), kind=kOutput, calls=%fused_computation.27 | convolution fusion | flops 337723392 | bytes 88246272 | tf_op jit(solution)/shard_map/bgsu,bugd->bgsd/dot_general | solution.py:29
  78.8 0.2 reshape.40
  79.0 0.0 copy-start.1
  79.0 0.0 copy-start
  79.0 8.0 %convolution_convert_fusion.1 = bf16[64,5120]{1,0:T(8,128)(2,1)} fusion(bf16[64,1280]{1,0:T(8,128)(2,1)S(1)} %reshape.40, bf16[1280,5120]{1,0:T(8,128)(2,1)} %param.15), kind=kOutput, calls=%fused_computation.2 | convolution fusion | flops 839188480 | bytes 13926400 | tf_op jit(solution)/shard_map/dot_general | solution.py:53
  87.0 0.1 all-reduce.3.cloned.1.call-update
  87.1 0.2 all-reduce.5.cloned.1.call-start
  87.4 0.0 copy-done.1
  87.4 38.1 %all-reduce.3.cloned.1.call-done = bf16[64,5120]{1,0:T(8,128)(2,1)} async-done(((bf16[64,5120]{1,0:T(8,128)(2,1)}), bf16[64,5120]{1,0:T(8,128)(2,1)}) %all-reduce.3.cloned.1.call-update) | async-done | bytes 655376 | tf_op jit(solution)/shard_map/psum | solution.py:49
  125.5 0.0 copy-done
  125.5 1.4 fusion.10
  126.9 14.4 %fusion.34 = f32[64,3456]{1,0:T(8,128)S(1)} fusion(bf16[5120,3456]{1,0:T(8,128)(2,1)} %param.17, bf16[64,5120]{1,0:T(8,128)(2,1)S(1)} %get-tuple-element.6, f32[5120]{0:T(1024)S(1)} %convert_element_type.74, f32[64]{0:T(128)S(1)} %add_rsqrt_fusion), kind=kOutput, calls=%fused_computation.48 | convolution fusion | flops 2266234880 | bytes 36950272 | tf_op jit(solution)/shard_map/dot_general | solution.py:42
  141.3 26.6 %convolution_convert_fusion = bf16[64,5120]{1,0:T(8,128)(2,1)} fusion(bf16[3456,5120]{1,0:T(8,128)(2,1)} %param.19, bf16[5120,3456]{1,0:T(8,128)(2,1)} %param.18, f32[64,3456]{1,0:T(8,128)S(1)} %fusion.34, bf16[64,5120]{1,0:T(8,128)(2,1)S(1)} %get-tuple-element.6, f32[5120]{0:T(1024)S(1)} %convert_element_type.74, f32[64]{0:T(128)S(1)} %add_rsqrt_fusion), kind=kOutput, calls=%fused_computation.1 | convolution fusion | flops 4532813824 | bytes 72995072 | tf_op jit(solution)/shard_map/dot_general | solution.py:54
  167.9 0.1 all-reduce.5.cloned.1.call-update
  167.9 36.0 %all-reduce.5.cloned.1.call-done = bf16[64,5120]{1,0:T(8,128)(2,1)} async-done(((bf16[64,5120]{1,0:T(8,128)(2,1)}), bf16[64,5120]{1,0:T(8,128)(2,1)}) %all-reduce.5.cloned.1.call-update) | async-done | bytes 655376 | tf_op jit(solution)/shard_map/psum | solution.py:49
  203.9 2.1 fusion.13
  (4 shorter events, 0.1 us)
Async XLA Ops:
  6.5 118.9 %all-reduce.3.cloned.1.call-start = ((), (), s32[]{:S(2)}) async-start(), calls=%async_computation | async-start | bytes 1310720 | tf_op jit(solution)/shard_map/psum | solution.py:49
  79.0 8.4 %copy-start.1 = (bf16[5120]{0:T(1024)(128)(2,1)S(1)}, bf16[5120]{0:T(1024)(128)(2,1)}, u32[]{:S(2)}) copy-start(bf16[5120]{0:T(1024)(128)(2,1)} %param.16) | copy-start | bytes 30724
  79.0 46.4 %copy-start = (bf16[64,5120]{1,0:T(8,128)(2,1)S(1)}, bf16[64,5120]{1,0:T(8,128)(2,1)}, u32[]{:S(2)}) copy-start(bf16[64,5120]{1,0:T(8,128)(2,1)} %param.10) | copy-start | bytes 1966084
  87.1 116.8 %all-reduce.5.cloned.1.call-start = ((), (), s32[]{:S(2)}) async-start(), calls=%async_computation.1 | async-start | bytes 1310720 | tf_op jit(solution)/shard_map/psum | solution.py:49
Sparse Core Ops, SparseCore 0:
  87.2 38.1 all-reduce.2
  168.1 35.8 all-reduce.4
where the time goes:
time: 213 us
  matrix products  119 us (56%)
  waiting for transfers between devices  74.2 us (35%)
  between operations  13.5 us (6%)
  other arithmetic  5.72 us (3%)
    psum x2, waiting for transfers between devices, added(): lax.psum(term.astype(jnp.bfloat16), 'tp').astype(jnp.float32)  74 us
    dot_general x1, matrix products, einsum(): return jnp.einsum(form, a.astype(jnp.float32), b.astype(jnp.float32))  31.9 us
    sub x1, matrix products, seen_by(): weights = jax.nn.softmax(scores, -1).astype(jnp.bfloat16)  30.2 us
    dot_general x1, matrix products, step(): jnp.dot(hidden_of(normed(h, gain_m), w_gate, w_up), w_down, preferred_ele...  26.6 us
    dot_general x1, matrix products, hidden_of(): gate = jnp.dot(b, w_gate, preferred_element_type=jnp.float32)  14.4 us
    dot_general x1, matrix products, step(): h = added(x, jnp.dot(seen, wo, preferred_element_type=jnp.float32))  8.01 us
    dot_general x1, matrix products, matmul(): jnp.dot(a, w, preferred_element_type=jnp.float32).astype(jnp.bfloat16)  7.41 us
  transfers between devices with their start and end apart: 2, of which 2 were waited for; matrix products, arithmetic and copies ran while one was open for 0% of the time, Pallas kernels for 0%

commit v1 on v0

v1 whole, which is shorter than its diff:
```python
import functools

import jax
import jax.numpy as jnp
import numpy as np
from jax import lax
from jax.experimental import pallas as pl
from jax.experimental.pallas import tpu as pltpu
from jax.sharding import PartitionSpec as P

HEAD = 160
THETA = 10000
F32, BF16 = jnp.float32, jnp.bfloat16
MESH = pl.DeviceIdType.MESH

BATCH = 4
RING = 3
UNIT = 1280
UNITS = 10
WIDE = 2048
SLAB = 320
CHUNK = 512
LOW = 1664
GROUPS = ((0, 12), (12, 16))
WO_AT = 6
SPLIT_UNIT = 8


def many(v, n):
    return pl.multiple_of(v, n)


def kernel(dims, x_hbm, k_hbm, v_hbm, ga_hbm, wq_hbm, wo_hbm, gm_hbm, wg_hbm, wu_hbm, wd_hbm, turn_hbm, out_hbm, *scratch):
    rows, d, cache, heads, kv_heads, ff = dims
    (pool, x_s, ga_s, gm_s, turn_s, ab, qs, os, seen, part, accu, st1, rv1, st2, rv2, h_s, y_s, hid, rv1b, st2b, rv2b,
     misc_sem, wq_sem, kv_sem, wo_sem, slab_sem, wd_sem, out_sem, a1_send, a1_recv, a2_send, a2_recv) = scratch
    kvd = kv_heads * HEAD
    tiles = -(-kvd // 128)
    qd = heads * HEAD
    share = heads // kv_heads
    batches = rows // BATCH
    slabs = d // SLAB
    chunks = d // CHUNK
    last = slabs - UNITS

    me = lax.axis_index("tp")
    beside = me + 1 - 2 * lax.rem(me, 2)
    across = 3 - me
    barrier = pltpu.get_barrier_semaphore()
    for other in (beside, across):
        pl.semaphore_signal(barrier, inc=1, device_id={"tp": other}, device_id_type=MESH)
    plan = (
        (beside, across, lax.rem((me + 1) // 2, 2), me // 2),
        (across, beside, me // 2, lax.rem(me, 2)),
    )

    x_copy = pltpu.make_async_copy(x_hbm, x_s, misc_sem.at[0])
    ga_copy = pltpu.make_async_copy(ga_hbm, ga_s, misc_sem.at[1])
    gm_copy = pltpu.make_async_copy(gm_hbm, gm_s, misc_sem.at[2])
    turn_copy = pltpu.make_async_copy(turn_hbm, turn_s, misc_sem.at[3])

    def wq_copy(i):
        return pltpu.make_async_copy(
            wq_hbm.at[pl.ds(i * UNIT, UNIT)], pool.at[pl.ds((WO_AT + i) * UNIT, UNIT), pl.ds(0, qd)], wq_sem.at[i]
        )

    def kv_at(i):
        return many(lax.rem(i + 2, RING) * (2 * UNIT), UNIT)

    def kv_copies(i):
        slot = lax.rem(i + 2, RING)
        n = BATCH * kvd
        return [
            pltpu.make_async_copy(src.at[pl.ds(many(i * n, n), n)], pool.at[pl.ds(kv_at(i) + j * UNIT, n)], kv_sem.at[slot, j])
            for j, src in enumerate((k_hbm, v_hbm))
        ]

    def wo_copies():
        return [
            pltpu.make_async_copy(
                wo_hbm.at[:, pl.ds(j * WIDE, w)], pool.at[pl.ds((WO_AT + j) * UNIT, qd), pl.ds(0, w)], wo_sem.at[j]
            )
            for j, w in enumerate((WIDE, WIDE, d - 2 * WIDE))
        ]

    def slab_copies(k):
        unit = lax.rem(k + UNITS - 1, UNITS)
        copies = []
        for m, src in enumerate((wg_hbm, wu_hbm)):
            for j, w in enumerate((WIDE, ff - WIDE)):
                p = 2 * m + j
                copies.append(
                    pltpu.make_async_copy(
                        src.at[pl.ds(many(k * SLAB, SLAB), SLAB), pl.ds(j * WIDE, w)],
                        pool.at[pl.ds(many(unit * UNIT, UNIT) + p * SLAB, SLAB), pl.ds(0, w)],
                        slab_sem.at[unit, p],
                    )
                )
        return copies

    def start(copies):
        for c in copies:
            c.start()

    def wait(copies, name):
        with jax.named_scope(name):
            for c in copies:
                c.wait()

    def chunk_place(pos):
        over4, over6 = (pos + 4) // 8, (pos + 2) // 8
        split = over4 - over6
        chunk = pos + 4 * split - 2 * over6
        row = UNIT * (5 * (1 - over4) + SPLIT_UNIT * split)
        lane = (pos - 4 * split - 6 * over6) * CHUNK
        return chunk, (row, lane), (row + LOW * (1 - split), lane + 2 * CHUNK * split)

    def chunk_copies(pos):
        chunk, low, high = chunk_place(pos)
        cols = pl.ds(many(chunk * CHUNK, CHUNK), CHUNK)
        return [
            pltpu.make_async_copy(
                wd_hbm.at[pl.ds(at, n), cols],
                pool.at[pl.ds(many(row, 128), n), pl.ds(many(lane, CHUNK), CHUNK)],
                wd_sem.at[pos, j],
            )
            for j, (at, n, (row, lane)) in enumerate(((0, LOW, low), (LOW, ff - LOW, high)))
        ]

    x_copy.start()
    ga_copy.start()
    turn_copy.start()
    for i in range(d // UNIT):
        wq_copy(i).start()
    for i in range(RING):
        start(kv_copies(i))
    gm_copy.start()

    @jax.named_scope("norm")
    def norm(src, gain_ref, row0, n):
        g = gain_ref[...].astype(F32)
        gain = jnp.concatenate([g[r : r + 1] for r in range(g.shape[0])], axis=1)

        def body(i, _):
            at = pl.ds(many(row0 + i * 16, 16), 16)
            wide = src[at, :].astype(F32)
            scale = lax.rsqrt(jnp.mean(wide * wide, -1, keepdims=True) + 1e-6)
            out = (wide * scale * gain).astype(BF16)
            for k in range(slabs):
                ab[k, at, :] = out[:, k * SLAB : (k + 1) * SLAB]
            return 0

        lax.fori_loop(0, n // 16, body, 0)

    x_copy.wait()
    ga_copy.wait()
    norm(x_s, ga_s, 0, rows)

    per = UNIT // SLAB
    for i in range(d // UNIT):
        wq_copy(i).wait()
        total = None
        for j in range(per):
            term = jnp.dot(
                ab[i * per + j], pool[(WO_AT + i) * UNIT + j * SLAB : (WO_AT + i) * UNIT + (j + 1) * SLAB, :qd],
                preferred_element_type=F32,
            )
            total = term if total is None else total + term
        part[:, :qd] = total if i == 0 else part[:, :qd] + total
    turn_copy.wait()
    cos, sin = turn_s[0:1, :], turn_s[1:2, :]
    blank = jnp.zeros((rows, HEAD), F32)
    for j in range(heads):
        t = part[:, j * HEAD : (j + 1) * HEAD].astype(BF16).astype(F32)
        swapped = jnp.concatenate([t[:, HEAD // 2 :], t[:, : HEAD // 2]], axis=1)
        t = (t * cos + swapped * sin).astype(BF16).astype(F32)
        side = [blank] * kv_heads
        side[j // share] = t
        t = jnp.concatenate(side + [jnp.zeros((rows, tiles * 128 - kvd), F32)], axis=1)
        for c in range(tiles):
            qs[c, pl.ds(j, rows, stride=heads), :] = t[:, c * 128 : (c + 1) * 128]

    half1, piece1, quarter1 = d // 2, d // 4, d // 8

    def first_copy(g, step, half):
        b0, b1 = GROUPS[g]
        at = pl.ds(b0 * BATCH, (b1 - b0) * BATCH)
        p1, p2, bit1, bit2 = plan[half]
        base = half * half1
        keep = base + bit1 * piece1
        if step == 0:
            src = st1.at[at, pl.ds(many(base + (1 - bit1) * piece1, 128), piece1)]
            dst, to = rv1.at[at, pl.ds(half * piece1, piece1)], p1
        elif step == 1:
            src = st2.at[at, pl.ds(half * quarter1, quarter1)]
            dst, to = rv2.at[at, pl.ds(half * quarter1, quarter1)], p2
        elif step == 2:
            src = dst = h_s.at[at, pl.ds(many(keep + bit2 * quarter1, 128), quarter1)]
            to = p2
        else:
            src = dst = h_s.at[at, pl.ds(many(keep, 128), piece1)]
            to = p1
        return pltpu.make_async_remote_copy(
            src_ref=src, dst_ref=dst, send_sem=a1_send.at[g, step, half], recv_sem=a1_recv.at[g, step, half],
            device_id={"tp": to}, device_id_type=MESH,
        )

    @jax.named_scope("first_step")
    def first_step(g, step):
        b0, b1 = GROUPS[g]
        at = slice(b0 * BATCH, b1 * BATCH)
        for half in range(2):
            p1, p2, bit1, bit2 = plan[half]
            base = half * half1
            keep = base + bit1 * piece1
            if step == 0:
                away = pl.ds(many(base + (1 - bit1) * piece1, 128), piece1)
                st1[at, away] = part[at, away].astype(BF16)
                first_copy(g, 0, half).start()
                continue
            first_copy(g, step - 1, half).wait_recv()
            if step == 1:
                off = (1 - bit2) * quarter1
                st2[at, half * quarter1 : (half + 1) * quarter1] = (
                    part[at, pl.ds(many(keep + off, 128), quarter1)]
                    + rv1[at, pl.ds(many(half * piece1 + off, 128), quarter1)].astype(F32)
                ).astype(BF16)
                first_copy(g, 1, half).start()
            elif step == 2:
                mine = pl.ds(many(keep + bit2 * quarter1, 128), quarter1)
                h_s[at, mine] = (
                    x_s[at, mine].astype(F32)
                    + part[at, mine]
                    + rv1[at, pl.ds(many(half * piece1 + bit2 * quarter1, 128), quarter1)].astype(F32)
                    + rv2[at, half * quarter1 : (half + 1) * quarter1].astype(F32)
                ).astype(BF16)
                first_copy(g, 2, half).start()
            elif step == 3:
                first_copy(g, 3, half).start()

    def first_sends(g):
        for half in range(2):
            for step in range(4):
                first_copy(g, step, half).wait_send()

    @jax.named_scope("project")
    def project(g):
        b0, b1 = GROUPS[g]
        n = (b1 - b0) * BATCH
        at = slice(b0 * BATCH, b1 * BATCH)
        for j in range(heads):
            o = jnp.concatenate([os[c, pl.ds(b0 * BATCH * heads + j, n, stride=heads), :] for c in range(tiles)], axis=1)
            h = j // share
            seen[at, j * HEAD : (j + 1) * HEAD] = o[:, h * HEAD : (h + 1) * HEAD].astype(BF16)
        lhs = seen[at, :]

        def body(c, _):
            row, lane = (WO_AT + c // 2) * UNIT, lax.rem(c, 2) * (WIDE // 2)
            w = pool[pl.ds(many(row, UNIT), qd), pl.ds(many(lane, WIDE // 2), WIDE // 2)]
            part[at, pl.ds(many(c * (WIDE // 2), WIDE // 2), WIDE // 2)] = jnp.dot(lhs, w, preferred_element_type=F32)
            return 0

        lax.fori_loop(0, d // (WIDE // 2), body, 0)

    def attend(i, _):
        wait(kv_copies(i), "kv_wait")
        at = kv_at(i)
        ws = []
        for j in range(BATCH):
            mine = pl.ds(many((i * BATCH + j) * heads, 8), heads)
            q = jnp.concatenate([qs[c, mine, :] for c in range(tiles)], axis=1)[:, :kvd].astype(BF16)
            scores = jnp.dot(q, pool[pl.ds(at + j * kvd, kvd), :], preferred_element_type=F32) * HEAD**-0.5
            top = jnp.max(scores, -1, keepdims=True)
            e = jnp.exp(scores - top)
            ws.append(e / jnp.sum(e, -1, keepdims=True))
        w = jnp.concatenate(ws, 0).astype(BF16)
        o = lax.dot_general(w, pool[pl.ds(at + UNIT, BATCH * kvd), :], (((1,), (1,)), ((), ())), preferred_element_type=F32)
        for j in range(BATCH):
            t = o[j * heads : (j + 1) * heads, j * kvd : (j + 1) * kvd]
            t = jnp.concatenate([t, jnp.zeros((heads, tiles * 128 - kvd), F32)], axis=1)
            for c in range(tiles):
                os[c, pl.ds(many((i * BATCH + j) * heads, 8), heads), :] = t[:, c * 128 : (c + 1) * 128]

        @pl.when(i + RING < batches)
        def _():
            start(kv_copies(i + RING))

        @pl.when(i == 5)
        def _():
            start(wo_copies())

        end0 = GROUPS[0][1]

        @pl.when(i == end0 - 1)
        def _():
            wait(wo_copies(), "wo_wait")
            project(0)
            pl.semaphore_wait(barrier, 2)
            first_step(0, 0)

        for step in range(1, 4):

            @pl.when(i == end0 - 1 + step)
            def _():
                first_step(0, step)

        @pl.when(i == batches - RING - 1)
        def _():
            start(slab_copies(0))

        @pl.when(i >= batches - RING)
        def _():
            k = 1 + 2 * (i - (batches - RING))
            start(slab_copies(k))
            start(slab_copies(k + 1))

        return 0

    lax.fori_loop(0, batches, attend, 0)

    project(1)
    first_step(1, 0)
    for k in range(2 * RING + 1, UNITS):
        start(slab_copies(k))
    for half in range(2):
        first_copy(0, 3, half).wait_recv()
    gm_copy.wait()
    b0, b1 = GROUPS[0]
    norm(h_s, gm_s, b0 * BATCH, (b1 - b0) * BATCH)
    for step in range(1, 4):
        first_step(1, step)
    accu[...] = jnp.zeros_like(accu)
    for half in range(2):
        first_copy(1, 3, half).wait_recv()
    first_sends(0)
    first_sends(1)
    part[:, :ff] = jnp.zeros((rows, ff), F32)
    b0, b1 = GROUPS[1]
    norm(h_s, gm_s, b0 * BATCH, (b1 - b0) * BATCH)

    def slab_body(k, _):
        unit = lax.rem(k + UNITS - 1, UNITS)
        wait(slab_copies(k), "slab_wait")
        lhs = ab[k]
        for m, acc in enumerate((part, accu)):
            for j, w in enumerate((WIDE, ff - WIDE)):
                at = pl.ds(many(unit * UNIT, UNIT) + (2 * m + j) * SLAB, SLAB)
                acc[:, j * WIDE : j * WIDE + w] += jnp.dot(lhs, pool[at, :w], preferred_element_type=F32)

        @pl.when(k < last)
        def _():
            start(slab_copies(k + UNITS))

        for after, first, n in ((8, 0, 4), (10, 4, 2), (13, 6, 4)):

            @pl.when(k == after)
            def _():
                for pos in range(first, first + n):
                    start(chunk_copies(pos))

        return 0

    lax.fori_loop(0, slabs, slab_body, 0)

    @jax.named_scope("hidden")
    def hidden_body(c, _):
        at = pl.ds(many(c * 384, 128), 384)
        hid[:, at] = (jax.nn.silu(part[:, at]) * accu[:, at]).astype(BF16)
        return 0

    lax.fori_loop(0, ff // 384, hidden_body, 0)

    side = CHUNK // 2

    def second_copy(pos, step, half):
        chunk, _, _ = chunk_place(pos)
        p1, p2, bit1, bit2 = plan[half]
        cols = pl.ds(many(chunk * CHUNK + half * side, side), side)
        if step == 0:
            src = st1.at[pl.ds(many((1 - bit1) * (rows // 2), 16), rows // 2), cols]
            dst, to = rv1b.at[pos, half], p1
        elif step == 1:
            src, dst, to = st2b.at[pos, half], rv2b.at[pos, half], p2
        elif step == 2:
            src = dst = y_s.at[pl.ds(many(bit1 * (rows // 2) + bit2 * (rows // 4), 16), rows // 4), cols]
            to = p2
        else:
            src = dst = y_s.at[pl.ds(many(bit1 * (rows // 2), 16), rows // 2), cols]
            to = p1
        return pltpu.make_async_remote_copy(
            src_ref=src, dst_ref=dst, send_sem=a2_send.at[pos, step, half], recv_sem=a2_recv.at[pos, step, half],
            device_id={"tp": to}, device_id_type=MESH,
        )

    @jax.named_scope("second_step")
    def second_step(pos, step):
        chunk, _, _ = chunk_place(pos)
        for half in range(2):
            p1, p2, bit1, bit2 = plan[half]
            cols = pl.ds(many(chunk * CHUNK + half * side, side), side)
            second_copy(pos, step - 1, half).wait_recv()
            if step == 1:
                off = (1 - bit2) * (rows // 4)
                st2b[pos, half] = (
                    part[pl.ds(many(bit1 * (rows // 2) + off, 16), rows // 4), cols]
                    + rv1b[pos, half, pl.ds(many(off, 16), rows // 4), :].astype(F32)
                ).astype(BF16)
                second_copy(pos, 1, half).start()
            elif step == 2:
                mine = pl.ds(many(bit1 * (rows // 2) + bit2 * (rows // 4), 16), rows // 4)
                y_s[mine, cols] = (
                    h_s[mine, cols].astype(F32)
                    + part[mine, cols]
                    + rv1b[pos, half, pl.ds(many(bit2 * (rows // 4), 16), rows // 4), :].astype(F32)
                    + rv2b[pos, half].astype(F32)
                ).astype(BF16)
                second_copy(pos, 2, half).start()
            elif step == 3:
                second_copy(pos, 3, half).start()

    def out_copy(pos):
        chunk, _, _ = chunk_place(pos)
        cols = pl.ds(many(chunk * CHUNK, CHUNK), CHUNK)
        return pltpu.make_async_copy(y_s.at[:, cols], out_hbm.at[:, cols], out_sem.at[pos])

    lag = 2

    def down_body(pos, _):
        @pl.when(pos >= 4 * lag)
        def _():
            done = pos - 4 * lag
            for half in range(2):
                second_copy(done, 3, half).wait_recv()
            out_copy(done).start()

        for step in (3, 2, 1):

            @pl.when((pos >= step * lag) & (pos < chunks + step * lag))
            def _():
                second_step(pos - step * lag, step)

        @pl.when(pos < chunks)
        def _():
            wait(chunk_copies(pos), "chunk_wait")
            chunk, (row, lane), (row_high, lane_high) = chunk_place(pos)
            total = jnp.dot(
                hid[:, :LOW], pool[pl.ds(many(row, 128), LOW), pl.ds(many(lane, CHUNK), CHUNK)], preferred_element_type=F32
            ) + jnp.dot(
                hid[:, LOW:],
                pool[pl.ds(many(row_high, 128), ff - LOW), pl.ds(many(lane_high, CHUNK), CHUNK)],
                preferred_element_type=F32,
            )
            cols = pl.ds(many(chunk * CHUNK, CHUNK), CHUNK)
            part[:, cols] = total
            for half in range(2):
                away = pl.ds(many((1 - plan[half][2]) * (rows // 2), 16), rows // 2)
                some = pl.ds(many(chunk * CHUNK + half * side, side), side)
                st1[away, some] = part[away, some].astype(BF16)
                second_copy(pos, 0, half).start()

        return 0

    lax.fori_loop(0, chunks + 4 * lag, down_body, 0)

    def finish(pos, _):
        out_copy(pos).wait()
        for half in range(2):
            for step in range(4):
                second_copy(pos, step, half).wait_send()
        return 0

    lax.fori_loop(0, chunks, finish, 0)


def solution(mesh):
    def step(x, k_cache, v_cache, gain_a, wq, wo, gain_m, w_gate, w_up, w_down):
        rows, d = x.shape
        _, cache, kv_heads, head = k_cache.shape
        heads, ff = wq.shape[1] // head, w_gate.shape[1]
        keys, values = (t.transpose(0, 2, 3, 1).reshape(rows * kv_heads * head, cache) for t in (k_cache, v_cache))
        half = head // 2
        angle = np.float32(cache - 1) * np.float32(THETA) ** (-np.arange(half, dtype=np.float32) / np.float32(half))
        cos, sin = np.cos(angle.astype(np.float32)), np.sin(angle.astype(np.float32))
        turn = np.zeros((8, head), np.float32)
        turn[0], turn[1] = np.concatenate([cos, cos]), np.concatenate([-sin, sin])
        chunks = d // CHUNK
        dims = (rows, d, cache, heads, kv_heads, ff)
        dma = pltpu.SemaphoreType.DMA
        return pl.pallas_call(
            functools.partial(kernel, dims),
            out_shape=jax.ShapeDtypeStruct((rows, d), BF16),
            in_specs=[pl.BlockSpec(memory_space=pltpu.HBM)] * 11,
            out_specs=pl.BlockSpec(memory_space=pltpu.HBM),
            scratch_shapes=[
                pltpu.VMEM((UNITS * UNIT, WIDE), BF16),
                pltpu.VMEM((rows, d), BF16),
                pltpu.VMEM((d // 128, 128), BF16),
                pltpu.VMEM((d // 128, 128), BF16),
                pltpu.VMEM((8, head), F32),
                pltpu.VMEM((d // SLAB, rows, SLAB), BF16),
                pltpu.VMEM((-(-kv_heads * head // 128), rows * heads, 128), F32),
                pltpu.VMEM((-(-kv_heads * head // 128), rows * heads, 128), F32),
                pltpu.VMEM((rows, heads * head), BF16),
                pltpu.VMEM((rows, d), F32),
                pltpu.VMEM((rows, ff), F32),
                pltpu.VMEM((rows, d), BF16),
                pltpu.VMEM((rows, d // 2), BF16),
                pltpu.VMEM((rows, d // 4), BF16),
                pltpu.VMEM((rows, d // 4), BF16),
                pltpu.VMEM((rows, d), BF16),
                pltpu.VMEM((rows, d), BF16),
                pltpu.VMEM((rows, ff), BF16),
                pltpu.VMEM((chunks, 2, rows // 2, CHUNK // 2), BF16),
                pltpu.VMEM((chunks, 2, rows // 4, CHUNK // 2), BF16),
                pltpu.VMEM((chunks, 2, rows // 4, CHUNK // 2), BF16),
                dma((4,)),
                dma((d // UNIT,)),
                dma((RING, 2)),
                dma((3,)),
                dma((UNITS, 4)),
                dma((chunks, 2)),
                dma((chunks,)),
                dma((2, 4, 2)),
                dma((2, 4, 2)),
                dma((chunks, 4, 2)),
                dma((chunks, 4, 2)),
            ],
            compiler_params=pltpu.CompilerParams(
                collective_id=0, has_side_effects=True, vmem_limit_bytes=67043328
            ),
        )(x, keys, values, gain_a.reshape(d // 128, 128), wq, wo, gain_m.reshape(d // 128, 128), w_gate, w_up, w_down, turn)

    states, cache, columns, rows_of = P("dp", None), P("dp", None, "tp", None), P(None, "tp"), P("tp", None)
    return jax.shard_map(
        step,
        mesh=mesh,
        in_specs=(states, cache, cache, P(None), columns, rows_of, P(None), columns, columns, rows_of),
        out_specs=states,
        check_vma=False,
    )
```

time: 213 us -> 139 us (0.65)
  Pallas kernels: 0 us -> 137 us
  matrix products: 119 us -> 0 us
  waiting for transfers between devices: 74.2 us -> 0 us
  between operations: 13.5 us -> 0.01 us
  other arithmetic: 5.72 us -> 0 us
    pallas_call x0 -> x1, Pallas kernels: none -> 137 us  [step(): pl.pallas_call(functools.partial(kernel, dims), out_shape=jax.ShapeDtypeS...]
    dot_general x5 -> x0, matrix products: 88.3 us -> none  [the longest x1 31.9 us: einsum(): return jnp.einsum(form, a.astype(jnp.float32), b.astype(jnp.float32))]
    psum x2 -> x0, waiting for transfers between devices: 74 us -> none  [added(): lax.psum(term.astype(jnp.bfloat16), 'tp').astype(jnp.float32)]
    sub x1 -> x0, matrix products: 30.2 us -> none  [seen_by(): weights = jax.nn.softmax(scores, -1).astype(jnp.bfloat16)]
    convert_element_type x3 -> x0, other arithmetic: 2.79 us -> none  [the longest x1 2.07 us: added(): (t.astype(jnp.float32) + lax.psum(term.astype(jnp.bfloat16), 'tp').astype...]
    reduce_sum x2 -> x0, other arithmetic: 2.73 us -> none  [normed(): scale = lax.rsqrt(jnp.mean(wide * wide, -1, keepdims=True) + 1e-06)]
  transfers between devices with their start and end apart: 2 -> 0, of which waited for: 2 -> 0; matrix products, arithmetic and copies ran while one was open for 0% -> 0% of each run, Pallas kernels for 0% -> 0%
where the time goes in v1:
time: 139 us
  Pallas kernels  137 us (99%)
  local copies, waits for them, and re-layouts  1.97 us (1%)
    pallas_call x1, Pallas kernels, step(): pl.pallas_call(functools.partial(kernel, dims), out_shape=jax.ShapeDtypeS...  137 us

profile of v1, /device:TPU:112, one launch (start us, length us, event | category | flops | bytes accessed | tf_op | source)
XLA Modules:
  0.0 138.9 jit_solution(15834948247278400468)
XLA Ops:
  0.0 136.9 %shard_map.109 = bf16[64,5120]{1,0:T(8,128)(2,1)} custom-call(bf16[64,5120]{1,0:T(8,128)(2,1)} %x_hbm.1, bf16[20480,2048]{1,0:T(8,128)(2,1)} %bitcast.1.k_hbm, bf16[20480,2048]{1,0:T(8,128)(2,1)} %bitcast.3.v_hbm, bf16[40,128]{1,0:T(8,128)(2,1)} %bitcast.8, bf16[5120,1280]{1,0:T(8,128)(2,1)} %wq_hbm.1, bf16[1280,5120]{1,0:T(8,128)(2,1)} %wo_hbm.1, ...), custom_call_target="tpu_custom_call" | custom-call | tf_op jit(solution)/shard_map/pallas_call | solution.py:489
  137.0 2.0 %copy.13 = bf16[64,5120]{1,0:T(8,128)(2,1)} copy(bf16[64,5120]{1,0:T(8,128)(2,1)} %shard_map.109) | data formatting | bytes 1310720

commit v2 on v0

v2 whole, which is shorter than its diff:
```python
import functools

import jax
import jax.numpy as jnp
import numpy as np
from jax import lax
from jax.experimental import pallas as pl
from jax.experimental.pallas import tpu as pltpu
from jax.sharding import PartitionSpec as P

HEAD = 160
THETA = 10000
F32, BF16 = jnp.float32, jnp.bfloat16
MESH = pl.DeviceIdType.MESH

BATCH = 4
RING = 3
UNIT = 1280
UNITS = 10
WIDE = 2048
PITCH = 2048
BLOCK = 1024
HALVED = 3
SLAB = 640
CHUNK = 512
GROUPS = ((0, 8), (8, 12), (12, 16))
WO_AT = 6
LAG = 5


def many(v, n):
    return pl.multiple_of(v, n)


def kernel(dims, x_hbm, k_hbm, v_hbm, ga_hbm, wq_hbm, wo_hbm, gm_hbm, wg_hbm, wu_hbm, wd_hbm, turn_hbm, y_s, *scratch):
    rows, d, cache, heads, kv_heads, ff = dims
    (pool, x_s, ga_s, gm_s, turn_s, ab, qs, seen, part, accu, sent, sent2, got1, got2, got1b,
     misc_sem, wq_sem, kv_sem, wo_sem, slab_sem, wd_sem, a1_send, a1_recv0, a1_recv1, a2_send, a2_recv, a2_more) = scratch
    kvd = kv_heads * HEAD
    tiles = -(-kvd // 128)
    qd = heads * HEAD
    share = heads // kv_heads
    batches = rows // BATCH
    slabs = d // SLAB
    chunks = d // CHUNK
    places = UNITS * UNIT // (4 * SLAB)

    me = lax.axis_index("tp")
    beside = me + 1 - 2 * lax.rem(me, 2)
    across = 3 - me
    barrier = pltpu.get_barrier_semaphore()
    for other in (beside, across):
        pl.semaphore_signal(barrier, inc=1, device_id={"tp": other}, device_id_type=MESH)
    plan = ((beside, across), (across, beside))
    bits = ((lax.rem((me + 1) // 2, 2), me // 2), (me // 2, lax.rem(me, 2)))

    x_copy = pltpu.make_async_copy(x_hbm, x_s, misc_sem.at[0])
    ga_copy = pltpu.make_async_copy(ga_hbm, ga_s, misc_sem.at[1])
    gm_copy = pltpu.make_async_copy(gm_hbm, gm_s, misc_sem.at[2])
    turn_copy = pltpu.make_async_copy(turn_hbm, turn_s, misc_sem.at[3])

    def wq_copy(i):
        return pltpu.make_async_copy(
            wq_hbm.at[pl.ds(i * UNIT, UNIT)], pool.at[pl.ds((WO_AT + i) * UNIT, UNIT), pl.ds(0, qd)], wq_sem.at[i]
        )

    def kv_at(i):
        return many(lax.rem(i + 2, RING) * (2 * UNIT), UNIT)

    def kv_copies(i):
        slot = lax.rem(i + 2, RING)
        n = BATCH * kvd
        return [
            pltpu.make_async_copy(
                src.at[pl.ds(many(i * n, n), n)], pool.at[pl.ds(kv_at(i) + j * UNIT, n), pl.ds(0, WIDE)], kv_sem.at[slot]
            )
            for j, src in enumerate((k_hbm, v_hbm))
        ]

    def wo_copies():
        return [
            pltpu.make_async_copy(
                wo_hbm.at[:, pl.ds(j * WIDE, w)], pool.at[pl.ds((WO_AT + j) * UNIT, qd), pl.ds(0, w)], wo_sem.at[0]
            )
            for j, w in enumerate((WIDE, WIDE, d - 2 * WIDE))
        ]

    def slab_copies(k):
        place = lax.rem(k, places)
        copies = []
        for m, src in enumerate((wg_hbm, wu_hbm)):
            for j, w in enumerate((WIDE, ff - WIDE)):
                p = 2 * m + j
                copies.append(
                    pltpu.make_async_copy(
                        src.at[pl.ds(many(k * SLAB, SLAB), SLAB), pl.ds(j * WIDE, w)],
                        pool.at[pl.ds(many(place * (4 * SLAB), SLAB) + p * SLAB, SLAB), pl.ds(0, w)],
                        slab_sem.at[place],
                    )
                )
        return copies

    def start(copies):
        for c in copies:
            c.start(priority=1)

    def wait(copy, name):
        with jax.named_scope(name):
            copy.wait()

    def pool_wait(words, sem, name):
        n = words // WIDE
        if n * WIDE == words:
            region = pool.at[pl.ds(0, n), pl.ds(0, WIDE)]
        else:
            region = pool.at[pl.ds(0, words // CHUNK), pl.ds(0, CHUNK)]
        wait(pltpu.make_async_copy(region, region, sem), name)

    per_wide = WIDE // CHUNK

    def chunk_place(c):
        group = c // per_wide
        first = 6 * (1 - (group + 1) // 2) + 3 * (group // 2)
        return many(first * UNIT, UNIT), many(lax.rem(c, per_wide) * CHUNK, CHUNK)

    def chunk_copy(c):
        row, lane = chunk_place(c)
        return pltpu.make_async_copy(
            wd_hbm.at[:, pl.ds(many(c * CHUNK, CHUNK), CHUNK)], pool.at[pl.ds(row, ff), pl.ds(lane, CHUNK)], wd_sem.at[c]
        )

    x_copy.start()
    ga_copy.start()
    turn_copy.start()
    for i in range(d // UNIT):
        wq_copy(i).start(priority=1)
    for i in range(RING):
        start(kv_copies(i))
    gm_copy.start()

    @jax.named_scope("norm")
    def norm(src, gain_ref, row0, n):
        g = gain_ref[...].astype(F32)
        gain = jnp.concatenate([g[r : r + 1] for r in range(g.shape[0])], axis=1)

        def body(i, _):
            at = pl.ds(many(row0 + i * 16, 16), 16)
            wide = src[at, :].astype(F32)
            scale = lax.rsqrt(jnp.mean(wide * wide, -1, keepdims=True) + 1e-6)
            out = (wide * scale * gain).astype(BF16)
            for k in range(slabs):
                ab[k, at, :] = out[:, k * SLAB : (k + 1) * SLAB]
            return 0

        lax.fori_loop(0, n // 16, body, 0)

    wait(x_copy, "x_wait")
    wait(ga_copy, "ga_wait")
    norm(x_s, ga_s, 0, rows)

    per = UNIT // SLAB
    for i in range(d // UNIT):
        wait(wq_copy(i), "wq_wait")
        total = None
        for j in range(per):
            term = jnp.dot(
                ab[i * per + j], pool[(WO_AT + i) * UNIT + j * SLAB : (WO_AT + i) * UNIT + (j + 1) * SLAB, :qd],
                preferred_element_type=F32,
            )
            total = term if total is None else total + term
        part[:, :qd] = total if i == 0 else part[:, :qd] + total
    wait(turn_copy, "turn_wait")
    cos, sin = turn_s[0:1, :], turn_s[1:2, :]
    blank = jnp.zeros((rows, HEAD), F32)
    for j in range(heads):
        t = part[:, j * HEAD : (j + 1) * HEAD].astype(BF16).astype(F32)
        swapped = jnp.concatenate([t[:, HEAD // 2 :], t[:, : HEAD // 2]], axis=1)
        t = (t * cos + swapped * sin).astype(BF16).astype(F32)
        side = [blank] * kv_heads
        side[j // share] = t
        t = jnp.concatenate(side + [jnp.zeros((rows, tiles * 128 - kvd), F32)], axis=1)
        for c in range(tiles):
            qs[c, pl.ds(j, rows, stride=heads), :] = t[:, c * 128 : (c + 1) * 128]

    def swap(step, half, at, got, send_sem, recv_sem):
        return pltpu.make_async_remote_copy(
            src_ref=(sent, sent2)[step].at[at], dst_ref=got[step].at[at], send_sem=send_sem, recv_sem=recv_sem,
            device_id={"tp": plan[half][step]}, device_id_type=MESH,
        )

    def arrived(words, sem):
        region = sent.at[:, pl.ds(0, words // rows)]
        pltpu.make_async_copy(region, region, sem).wait()

    half_block = BLOCK // 2
    exposed = len(GROUPS) - 1

    def rows_of(g):
        b0, b1 = GROUPS[g]
        return b0 * BATCH, (b1 - b0) * BATCH

    def first_recv(g, step, c):
        return a1_recv1.at[step, c] if g == exposed else a1_recv0.at[step, g]

    def first_send(g, step, c):
        row0, n = rows_of(g)
        for half in range(2):
            at = (pl.ds(row0, n), pl.ds(many(c * BLOCK + half * half_block, half_block), half_block))
            swap(step, half, at, (got1, got2), a1_send.at[step], first_recv(g, step, c)).start()

    def first_step(g, step, c):
        row0, n = rows_of(g)
        at = (pl.ds(row0, n), pl.ds(many(c * BLOCK, BLOCK), BLOCK))
        if g == exposed:
            with jax.named_scope("first_wait"):
                arrived(n * BLOCK, first_recv(g, step, c))
        if step == 0:
            sent2[at] = (sent[at].astype(F32) + got1[at].astype(F32)).astype(BF16)
            first_send(g, 1, c)
        else:
            x_s[at] = (x_s[at].astype(F32) + (sent2[at].astype(F32) + got2[at].astype(F32))).astype(BF16)

    def all_blocks(g, step):
        row0, n = rows_of(g)
        with jax.named_scope("all_wait"):
            arrived(n * d, first_recv(g, step, 0))
        lax.fori_loop(0, d // BLOCK, lambda c, _: first_step(g, step, c) or 0, 0)

    @jax.named_scope("gather_seen")
    def gather_seen(g):
        row0, n = rows_of(g)
        for j in range(heads):
            o = jnp.concatenate([qs[c, pl.ds(row0 * heads + j, n, stride=heads), :] for c in range(tiles)], axis=1)
            h = j // share
            seen[row0 : row0 + n, j * HEAD : (j + 1) * HEAD] = o[:, h * HEAD : (h + 1) * HEAD].astype(BF16)

    @jax.named_scope("project")
    def project(g, c):
        row0, n = rows_of(g)
        row, lane = (WO_AT + c // 2) * UNIT, lax.rem(c, 2) * BLOCK
        w = pool[pl.ds(many(row, UNIT), qd), pl.ds(many(lane, BLOCK), BLOCK)]
        at = (slice(row0, row0 + n), pl.ds(many(c * BLOCK, BLOCK), BLOCK))
        sent[at] = jnp.dot(seen[row0 : row0 + n, :], w, preferred_element_type=F32).astype(BF16)
        first_send(g, 0, c)

    def attend(i, _):
        pool_wait(2 * BATCH * kvd * WIDE, kv_sem.at[lax.rem(i + 2, RING)], "kv_wait")
        at = kv_at(i)
        ws = []
        for j in range(BATCH):
            mine = pl.ds(many((i * BATCH + j) * heads, 8), heads)
            q = jnp.concatenate([qs[c, mine, :] for c in range(tiles)], axis=1)[:, :kvd].astype(BF16)
            scores = jnp.dot(q, pool[pl.ds(at + j * kvd, kvd), :WIDE], preferred_element_type=F32) * HEAD**-0.5
            top = jnp.max(scores, -1, keepdims=True)
            e = jnp.exp(scores - top)
            ws.append(e / jnp.sum(e, -1, keepdims=True))
        w = jnp.concatenate(ws, 0).astype(BF16)
        o = lax.dot_general(w, pool[pl.ds(at + UNIT, BATCH * kvd), :WIDE], (((1,), (1,)), ((), ())), preferred_element_type=F32)
        for j in range(BATCH):
            t = o[j * heads : (j + 1) * heads, j * kvd : (j + 1) * kvd]
            t = jnp.concatenate([t, jnp.zeros((heads, tiles * 128 - kvd), F32)], axis=1)
            for c in range(tiles):
                qs[c, pl.ds(many((i * BATCH + j) * heads, 8), heads), :] = t[:, c * 128 : (c + 1) * 128]

        @pl.when(i + RING < batches)
        def _():
            start(kv_copies(i + RING))

        @pl.when(i == 3)
        def _():
            start(wo_copies())

        @pl.when(i >= batches - RING)
        def _():
            start(slab_copies(i - (batches - RING)))

        end0, end1 = GROUPS[0][1], GROUPS[1][1]

        @pl.when(i == end0 - 1)
        def _():
            pool_wait(qd * d, wo_sem.at[0], "wo_wait")
            pl.semaphore_wait(barrier, 2)

        for g, end in enumerate((end0, end1)):

            @pl.when(i == end - 1)
            def _():
                gather_seen(g)
                lax.fori_loop(0, d // BLOCK, lambda c, _: project(g, c) or 0, 0)

            @pl.when(i == end + 2)
            def _():
                all_blocks(g, 0)

        @pl.when(i == end0 + 5)
        def _():
            all_blocks(0, 1)
            gm_copy.wait()
            norm(x_s, gm_s, *rows_of(0))

        return 0

    lax.fori_loop(0, batches, attend, 0)

    gather_seen(exposed)
    blocks = d // BLOCK

    def project_body(c, _):
        project(exposed, c)

        @pl.when(c == blocks - 1)
        def _():
            for k in range(RING, places):
                start(slab_copies(k))

        return 0

    lax.fori_loop(0, blocks, project_body, 0)
    all_blocks(exposed - 1, 1)
    norm(x_s, gm_s, *rows_of(exposed - 1))
    accu[...] = jnp.zeros_like(accu)
    part[:, :ff] = jnp.zeros((rows, ff), F32)
    for step in range(2):
        lax.fori_loop(0, blocks, lambda c, _: first_step(exposed, step, c) or 0, 0)
    norm(x_s, gm_s, *rows_of(exposed))
    for step in range(2):
        arrived(rows * d, a1_send.at[step])

    def slab_body(k, _):
        place = lax.rem(k, places)
        pool_wait(2 * SLAB * ff, slab_sem.at[place], "slab_wait")
        lhs = ab[k]
        for m, acc in enumerate((part, accu)):
            for j, w in enumerate((WIDE, ff - WIDE)):
                at = pl.ds(many(place * (4 * SLAB), SLAB) + (2 * m + j) * SLAB, SLAB)
                acc[:, j * WIDE : j * WIDE + w] += jnp.dot(lhs, pool[at, :w], preferred_element_type=F32)

        @pl.when(k < slabs - places)
        def _():
            start(slab_copies(k + places))

        for after, first, last in ((4, 0, per_wide), (6, per_wide, 2 * per_wide), (7, 2 * per_wide, chunks)):

            @pl.when(k == after)
            def _():
                for c in range(first, last):
                    start([chunk_copy(c)])

        return 0

    lax.fori_loop(0, slabs, slab_body, 0)

    def hidden_body(c, _):
        at = pl.ds(many(c * 384, 128), 384)
        got1[:, at] = (jax.nn.silu(part[:, at]) * accu[:, at]).astype(BF16)
        return 0

    lax.fori_loop(0, ff // 384, hidden_body, 0)

    side = CHUNK // 2
    row2, row4 = rows // 2, rows // 4

    def columns_of(c, half):
        return pl.ds(many(c * CHUNK + half * side, side), side)

    def chunk_recv(c, step):
        return a2_recv.at[c, step] if step < 2 else a2_more.at[c, step - 2]

    def full_send(c, step):
        for half in range(2):
            at = (slice(None), columns_of(c, half))
            swap(step, half, at, (got1b, y_s), a2_send.at[step], chunk_recv(c, step)).start()

    @jax.named_scope("full_step")
    def full_step(c, step):
        arrived(rows * CHUNK, chunk_recv(c, step))
        at = (slice(None), pl.ds(many(c * CHUNK, CHUNK), CHUNK))
        if step == 0:
            sent2[at] = (sent[at].astype(F32) + got1b[at].astype(F32)).astype(BF16)
            full_send(c, 1)
        else:
            y_s[at] = (x_s[at].astype(F32) + (sent2[at].astype(F32) + y_s[at].astype(F32))).astype(BF16)

    def halved_send(c, step, half):
        bit1, bit2 = bits[half]
        row, n, src, dst, to = (
            ((1 - bit1) * row2, row2, sent, got1b, 0),
            (bit1 * row2 + (1 - bit2) * row4, row4, sent2, y_s, 1),
            (bit1 * row2 + bit2 * row4, row4, y_s, y_s, 1),
            (bit1 * row2, row2, y_s, y_s, 0),
        )[step]
        at = (pl.ds(many(row, 16), n), columns_of(c, half))
        pltpu.make_async_remote_copy(
            src_ref=src.at[at], dst_ref=dst.at[at], send_sem=a2_send.at[step], recv_sem=chunk_recv(c, step),
            device_id={"tp": plan[half][to]}, device_id_type=MESH,
        ).start()

    @jax.named_scope("halved_step")
    def halved_step(c, step):
        arrived((row2, row4, row4, row2)[step] * CHUNK, chunk_recv(c, step))
        for half in range(2):
            bit1, bit2 = bits[half]
            cols = columns_of(c, half)
            if step == 0:
                at = (pl.ds(many(bit1 * row2 + (1 - bit2) * row4, 16), row4), cols)
                sent2[at] = (part[at] + got1b[at].astype(F32)).astype(BF16)
            elif step == 1:
                at = (pl.ds(many(bit1 * row2 + bit2 * row4, 16), row4), cols)
                y_s[at] = (
                    x_s[at].astype(F32) + (part[at] + got1b[at].astype(F32) + y_s[at].astype(F32))
                ).astype(BF16)
            if step < 3:
                halved_send(c, step + 1, half)

    def down(i):
        wait(chunk_copy(i), "chunk_wait")
        row, lane = chunk_place(i)
        return jnp.dot(got1[:, :ff], pool[pl.ds(row, ff), pl.ds(lane, CHUNK)], preferred_element_type=F32)

    def down_body(i, _):
        for step in (3, 2, 1, 0):
            at = (step + 1) * LAG

            @pl.when((i >= at) & (i < HALVED + at))
            def _():
                halved_step(i - at, step)

            if step < 2:

                @pl.when((i >= HALVED + at) & (i < chunks + at))
                def _():
                    full_step(i - at, step)

        @pl.when(i < HALVED)
        def _():
            cols = pl.ds(many(i * CHUNK, CHUNK), CHUNK)
            part[:, cols] = down(i)
            for half in range(2):
                at = (pl.ds(many((1 - bits[half][0]) * row2, 16), row2), columns_of(i, half))
                sent[at] = part[at].astype(BF16)
                halved_send(i, 0, half)

        @pl.when((i >= HALVED) & (i < chunks))
        def _():
            sent[:, pl.ds(many(i * CHUNK, CHUNK), CHUNK)] = down(i).astype(BF16)
            full_send(i, 0)

        return 0

    lax.fori_loop(0, max(chunks + 2 * LAG, HALVED + 4 * LAG), down_body, 0)
    whole = chunks - HALVED
    for step, n in enumerate((HALVED * row2 + whole * rows, HALVED * row4 + whole * rows, HALVED * row4, HALVED * row2)):
        arrived(n * CHUNK, a2_send.at[step])


def solution(mesh):
    def step(x, k_cache, v_cache, gain_a, wq, wo, gain_m, w_gate, w_up, w_down):
        rows, d = x.shape
        _, cache, kv_heads, head = k_cache.shape
        heads, ff = wq.shape[1] // head, w_gate.shape[1]
        keys, values = (t.transpose(0, 2, 3, 1).reshape(rows * kv_heads * head, cache) for t in (k_cache, v_cache))
        half = head // 2
        angle = np.float32(cache - 1) * np.float32(THETA) ** (-np.arange(half, dtype=np.float32) / np.float32(half))
        cos, sin = np.cos(angle.astype(np.float32)), np.sin(angle.astype(np.float32))
        turn = np.zeros((8, head), np.float32)
        turn[0], turn[1] = np.concatenate([cos, cos]), np.concatenate([-sin, sin])
        chunks = d // CHUNK
        dims = (rows, d, cache, heads, kv_heads, ff)
        dma = pltpu.SemaphoreType.DMA
        return pl.pallas_call(
            functools.partial(kernel, dims),
            out_shape=pltpu.VMEM((rows, d), BF16),
            in_specs=[pl.BlockSpec(memory_space=pltpu.HBM)] * 11,
            out_specs=pl.BlockSpec(memory_space=pltpu.VMEM),
            scratch_shapes=[
                pltpu.VMEM((UNITS * UNIT, PITCH), BF16),
                pltpu.VMEM((rows, d), BF16),
                pltpu.VMEM((d // 128, 128), BF16),
                pltpu.VMEM((d // 128, 128), BF16),
                pltpu.VMEM((8, head), F32),
                pltpu.VMEM((d // SLAB, rows, SLAB), BF16),
                pltpu.VMEM((-(-kv_heads * head // 128), rows * heads, 128), F32),
                pltpu.VMEM((rows, heads * head), BF16),
                pltpu.VMEM((rows, d), F32),
                pltpu.VMEM((rows, ff), F32),
                pltpu.VMEM((rows, d), BF16),
                pltpu.VMEM((rows, d), BF16),
                pltpu.VMEM((rows, d), BF16),
                pltpu.VMEM((rows, d), BF16),
                pltpu.VMEM((rows, d), BF16),
                dma((4,)),
                dma((d // UNIT,)),
                dma((RING,)),
                dma((1,)),
                dma((UNITS * UNIT // (4 * SLAB),)),
                dma((chunks,)),
                dma((2,)),
                dma((2, len(GROUPS) - 1)),
                dma((2, d // BLOCK)),
                dma((4,)),
                dma((chunks, 2)),
                dma((HALVED, 2)),
            ],
            compiler_params=pltpu.CompilerParams(
                collective_id=0, has_side_effects=True, vmem_limit_bytes=66350000
            ),
        )(x, keys, values, gain_a.reshape(d // 128, 128), wq, wo, gain_m.reshape(d // 128, 128), w_gate, w_up, w_down, turn)

    states, cache, columns, rows_of = P("dp", None), P("dp", None, "tp", None), P(None, "tp"), P("tp", None)
    return jax.shard_map(
        step,
        mesh=mesh,
        in_specs=(states, cache, cache, P(None), columns, rows_of, P(None), columns, columns, rows_of),
        out_specs=states,
        check_vma=False,
    )
```

time: 213 us -> 108 us (0.51)
  matrix products: 119 us -> 0 us
  Pallas kernels: 0 us -> 107 us
  waiting for transfers between devices: 74.2 us -> 0 us
  between operations: 13.5 us -> 0.01 us
  other arithmetic: 5.72 us -> 0 us
    pallas_call x0 -> x1, Pallas kernels: none -> 107 us  [step(): pl.pallas_call(functools.partial(kernel, dims), out_shape=pltpu.VMEM((row...]
    dot_general x5 -> x0, matrix products: 88.3 us -> none  [the longest x1 31.9 us: einsum(): return jnp.einsum(form, a.astype(jnp.float32), b.astype(jnp.float32))]
    psum x2 -> x0, waiting for transfers between devices: 74 us -> none  [added(): lax.psum(term.astype(jnp.bfloat16), 'tp').astype(jnp.float32)]
    sub x1 -> x0, matrix products: 30.2 us -> none  [seen_by(): weights = jax.nn.softmax(scores, -1).astype(jnp.bfloat16)]
    convert_element_type x3 -> x0, other arithmetic: 2.79 us -> none  [the longest x1 2.07 us: added(): (t.astype(jnp.float32) + lax.psum(term.astype(jnp.bfloat16), 'tp').astype...]
    reduce_sum x2 -> x0, other arithmetic: 2.73 us -> none  [normed(): scale = lax.rsqrt(jnp.mean(wide * wide, -1, keepdims=True) + 1e-06)]
  transfers between devices with their start and end apart: 2 -> 0, of which waited for: 2 -> 0; matrix products, arithmetic and copies ran while one was open for 0% -> 0% of each run, Pallas kernels for 0% -> 0%
where the time goes in v2:
time: 108 us
  Pallas kernels  107 us (99%)
    pallas_call x1, Pallas kernels, step(): pl.pallas_call(functools.partial(kernel, dims), out_shape=pltpu.VMEM((row...  107 us

profile of v2, /device:TPU:112, one launch (start us, length us, event | category | flops | bytes accessed | tf_op | source)
XLA Modules:
  0.0 107.8 jit_solution(7619633276811224207)
XLA Ops:
  0.0 107.0 %shard_map.109 = bf16[64,5120]{1,0:T(8,128)(2,1)S(1)} custom-call(bf16[64,5120]{1,0:T(8,128)(2,1)} %x_hbm.1, bf16[20480,2048]{1,0:T(8,128)(2,1)} %bitcast.1.k_hbm, bf16[20480,2048]{1,0:T(8,128)(2,1)} %bitcast.3.v_hbm, bf16[40,128]{1,0:T(8,128)(2,1)} %bitcast.8, bf16[5120,1280]{1,0:T(8,128)(2,1)} %wq_hbm.1, bf16[1280,5120]{1,0:T(8,128)(2,1)} %wo_hbm.1, ...), custom_call_target="tpu_custom_call" | custom-call | tf_op jit(solution)/shard_map/pallas_call | solution.py:470
  107.0 0.8 copy.13

commit v3 on v2

--- a/solution.py
+++ b/solution.py
@@ -20,11 +20,13 @@
 WIDE = 2048
 PITCH = 2048
 BLOCK = 1024
-HALVED = 3
 SLAB = 640
 CHUNK = 512
-GROUPS = ((0, 8), (8, 12), (12, 16))
+GROUPS = ((0, 12), (12, 16))
 WO_AT = 6
+EARLY = 3
+WO_SEM = 4
+HALVED = 6
 LAG = 5
 
 
@@ -35,7 +37,7 @@
 def kernel(dims, x_hbm, k_hbm, v_hbm, ga_hbm, wq_hbm, wo_hbm, gm_hbm, wg_hbm, wu_hbm, wd_hbm, turn_hbm, y_s, *scratch):
     rows, d, cache, heads, kv_heads, ff = dims
     (pool, x_s, ga_s, gm_s, turn_s, ab, qs, seen, part, accu, sent, sent2, got1, got2, got1b,
-     misc_sem, wq_sem, kv_sem, wo_sem, slab_sem, wd_sem, a1_send, a1_recv0, a1_recv1, a2_send, a2_recv, a2_more) = scratch
+     misc_sem, flow, kv_sem, a1_send, a1_recv0, a1_recv1, a2_send, a2_recv, a2_back) = scratch
     kvd = kv_heads * HEAD
     tiles = -(-kvd // 128)
     qd = heads * HEAD
@@ -52,7 +54,8 @@
     for other in (beside, across):
         pl.semaphore_signal(barrier, inc=1, device_id={"tp": other}, device_id_type=MESH)
     plan = ((beside, across), (across, beside))
-    bits = ((lax.rem((me + 1) // 2, 2), me // 2), (me // 2, lax.rem(me, 2)))
+    kept = (lax.rem((me + 1) // 2, 2), me // 2)
+
 
     x_copy = pltpu.make_async_copy(x_hbm, x_s, misc_sem.at[0])
     ga_copy = pltpu.make_async_copy(ga_hbm, ga_s, misc_sem.at[1])
@@ -61,7 +64,7 @@
 
     def wq_copy(i):
         return pltpu.make_async_copy(
-            wq_hbm.at[pl.ds(i * UNIT, UNIT)], pool.at[pl.ds((WO_AT + i) * UNIT, UNIT), pl.ds(0, qd)], wq_sem.at[i]
+            wq_hbm.at[pl.ds(i * UNIT, UNIT)], pool.at[pl.ds((WO_AT + i) * UNIT, UNIT), pl.ds(0, qd)], flow.at[i]
         )
 
     def kv_at(i):
@@ -72,7 +75,7 @@
         n = BATCH * kvd
         return [
             pltpu.make_async_copy(
-                src.at[pl.ds(many(i * n, n), n)], pool.at[pl.ds(kv_at(i) + j * UNIT, n), pl.ds(0, WIDE)], kv_sem.at[slot]
+                src.at[pl.ds(many(i * n, n), n)], pool.at[pl.ds(kv_at(i) + j * UNIT, n), pl.ds(0, WIDE)], kv_sem.at[slot, j]
             )
             for j, src in enumerate((k_hbm, v_hbm))
         ]
@@ -80,10 +83,13 @@
     def wo_copies():
         return [
             pltpu.make_async_copy(
-                wo_hbm.at[:, pl.ds(j * WIDE, w)], pool.at[pl.ds((WO_AT + j) * UNIT, qd), pl.ds(0, w)], wo_sem.at[0]
+                wo_hbm.at[:, pl.ds(j * WIDE, w)], pool.at[pl.ds((WO_AT + j) * UNIT, qd), pl.ds(0, w)], flow.at[WO_SEM]
             )
             for j, w in enumerate((WIDE, WIDE, d - 2 * WIDE))
         ]
+
+    def slab_sem(place):
+        return flow.at[WO_SEM + 1 + lax.rem(place + 2, places)]
 
     def slab_copies(k):
         place = lax.rem(k, places)
@@ -95,7 +101,7 @@
                     pltpu.make_async_copy(
                         src.at[pl.ds(many(k * SLAB, SLAB), SLAB), pl.ds(j * WIDE, w)],
                         pool.at[pl.ds(many(place * (4 * SLAB), SLAB) + p * SLAB, SLAB), pl.ds(0, w)],
-                        slab_sem.at[place],
+                        slab_sem(place),
                     )
                 )
         return copies
@@ -126,7 +132,7 @@
     def chunk_copy(c):
         row, lane = chunk_place(c)
         return pltpu.make_async_copy(
-            wd_hbm.at[:, pl.ds(many(c * CHUNK, CHUNK), CHUNK)], pool.at[pl.ds(row, ff), pl.ds(lane, CHUNK)], wd_sem.at[c]
+            wd_hbm.at[:, pl.ds(many(c * CHUNK, CHUNK), CHUNK)], pool.at[pl.ds(row, ff), pl.ds(lane, CHUNK)], flow.at[c]
         )
 
     x_copy.start()
@@ -243,8 +249,15 @@
         sent[at] = jnp.dot(seen[row0 : row0 + n, :], w, preferred_element_type=F32).astype(BF16)
         first_send(g, 0, c)
 
-    def attend(i, _):
-        pool_wait(2 * BATCH * kvd * WIDE, kv_sem.at[lax.rem(i + 2, RING)], "kv_wait")
+    def attend(i, early):
+        slot = lax.rem(i + 2, RING)
+
+        def kv_wait(j, name):
+            pool_wait(BATCH * kvd * WIDE, kv_sem.at[slot, j], name)
+
+        kv_wait(0, "k_wait")
+        if not early:
+            kv_wait(1, "v_wait")
         at = kv_at(i)
         ws = []
         for j in range(BATCH):
@@ -255,6 +268,8 @@
             e = jnp.exp(scores - top)
             ws.append(e / jnp.sum(e, -1, keepdims=True))
         w = jnp.concatenate(ws, 0).astype(BF16)
+        if early:
+            kv_wait(1, "v_wait")
         o = lax.dot_general(w, pool[pl.ds(at + UNIT, BATCH * kvd), :WIDE], (((1,), (1,)), ((), ())), preferred_element_type=F32)
         for j in range(BATCH):
             t = o[j * heads : (j + 1) * heads, j * kvd : (j + 1) * kvd]
@@ -266,7 +281,7 @@
         def _():
             start(kv_copies(i + RING))
 
-        @pl.when(i == 3)
+        @pl.when(i == 6)
         def _():
             start(wo_copies())
 
@@ -274,33 +289,23 @@
         def _():
             start(slab_copies(i - (batches - RING)))
 
-        end0, end1 = GROUPS[0][1], GROUPS[1][1]
+        end0 = GROUPS[0][1]
 
         @pl.when(i == end0 - 1)
         def _():
-            pool_wait(qd * d, wo_sem.at[0], "wo_wait")
+            pool_wait(qd * d, flow.at[WO_SEM], "wo_wait")
             pl.semaphore_wait(barrier, 2)
-
-        for g, end in enumerate((end0, end1)):
-
-            @pl.when(i == end - 1)
-            def _():
-                gather_seen(g)
-                lax.fori_loop(0, d // BLOCK, lambda c, _: project(g, c) or 0, 0)
-
-            @pl.when(i == end + 2)
-            def _():
-                all_blocks(g, 0)
-
-        @pl.when(i == end0 + 5)
-        def _():
-            all_blocks(0, 1)
-            gm_copy.wait()
-            norm(x_s, gm_s, *rows_of(0))
-
-        return 0
-
-    lax.fori_loop(0, batches, attend, 0)
+            gather_seen(0)
+            lax.fori_loop(0, d // BLOCK, lambda c, _: project(0, c) or 0, 0)
+
+        @pl.when(i == end0 + 1)
+        def _():
+            all_blocks(0, 0)
+
+        return 0
+
+    lax.fori_loop(0, GROUPS[0][1], lambda i, _: attend(i, True), 0)
+    lax.fori_loop(GROUPS[0][1], batches, lambda i, _: attend(i, False), 0)
 
     gather_seen(exposed)
     blocks = d // BLOCK
@@ -317,24 +322,25 @@
 
     lax.fori_loop(0, blocks, project_body, 0)
     all_blocks(exposed - 1, 1)
+    gm_copy.wait()
     norm(x_s, gm_s, *rows_of(exposed - 1))
     accu[...] = jnp.zeros_like(accu)
     part[:, :ff] = jnp.zeros((rows, ff), F32)
-    for step in range(2):
-        lax.fori_loop(0, blocks, lambda c, _: first_step(exposed, step, c) or 0, 0)
-    norm(x_s, gm_s, *rows_of(exposed))
-    for step in range(2):
-        arrived(rows * d, a1_send.at[step])
-
-    def slab_body(k, _):
+
+    @jax.named_scope("slab")
+    def slab_dots(k, row0, n):
         place = lax.rem(k, places)
-        pool_wait(2 * SLAB * ff, slab_sem.at[place], "slab_wait")
-        lhs = ab[k]
+        mine = slice(row0, row0 + n)
+        lhs = ab[k, mine, :]
         for m, acc in enumerate((part, accu)):
             for j, w in enumerate((WIDE, ff - WIDE)):
                 at = pl.ds(many(place * (4 * SLAB), SLAB) + (2 * m + j) * SLAB, SLAB)
-                acc[:, j * WIDE : j * WIDE + w] += jnp.dot(lhs, pool[at, :w], preferred_element_type=F32)
-
+                acc[mine, j * WIDE : j * WIDE + w] += jnp.dot(lhs, pool[at, :w], preferred_element_type=F32)
+
+    def slab_wait(k):
+        pool_wait(2 * SLAB * ff, slab_sem(lax.rem(k, places)), "slab_wait")
+
+    def refill(k):
         @pl.when(k < slabs - places)
         def _():
             start(slab_copies(k + places))
@@ -346,9 +352,38 @@
                 for c in range(first, last):
                     start([chunk_copy(c)])
 
-        return 0
-
-    lax.fori_loop(0, slabs, slab_body, 0)
+    last_row, last_rows = rows_of(exposed)
+
+    def early_body(k, _):
+        slab_wait(k)
+        slab_dots(k, 0, last_row)
+
+        @pl.when(k == 0)
+        def _():
+            lax.fori_loop(0, blocks, lambda c, _: first_step(exposed, 0, c) or 0, 0)
+
+        return 0
+
+    lax.fori_loop(0, EARLY, early_body, 0)
+    lax.fori_loop(0, blocks, lambda c, _: first_step(exposed, 1, c) or 0, 0)
+    norm(x_s, gm_s, last_row, last_rows)
+    for step in range(2):
+        arrived(rows * d, a1_send.at[step])
+
+    def late_body(k, _):
+        slab_dots(k, last_row, last_rows)
+        refill(k)
+        return 0
+
+    lax.fori_loop(0, EARLY, late_body, 0)
+
+    def slab_body(k, _):
+        slab_wait(k)
+        slab_dots(k, 0, rows)
+        refill(k)
+        return 0
+
+    lax.fori_loop(EARLY, slabs, slab_body, 0)
 
     def hidden_body(c, _):
         at = pl.ds(many(c * 384, 128), 384)
@@ -358,22 +393,18 @@
     lax.fori_loop(0, ff // 384, hidden_body, 0)
 
     side = CHUNK // 2
-    row2, row4 = rows // 2, rows // 4
 
     def columns_of(c, half):
         return pl.ds(many(c * CHUNK + half * side, side), side)
-
-    def chunk_recv(c, step):
-        return a2_recv.at[c, step] if step < 2 else a2_more.at[c, step - 2]
 
     def full_send(c, step):
         for half in range(2):
             at = (slice(None), columns_of(c, half))
-            swap(step, half, at, (got1b, y_s), a2_send.at[step], chunk_recv(c, step)).start()
+            swap(step, half, at, (got1b, y_s), a2_send.at[step], a2_recv.at[c, step]).start()
 
     @jax.named_scope("full_step")
     def full_step(c, step):
-        arrived(rows * CHUNK, chunk_recv(c, step))
+        arrived(rows * CHUNK, a2_recv.at[c, step])
         at = (slice(None), pl.ds(many(c * CHUNK, CHUNK), CHUNK))
         if step == 0:
             sent2[at] = (sent[at].astype(F32) + got1b[at].astype(F32)).astype(BF16)
@@ -381,36 +412,30 @@
         else:
             y_s[at] = (x_s[at].astype(F32) + (sent2[at].astype(F32) + y_s[at].astype(F32))).astype(BF16)
 
-    def halved_send(c, step, half):
-        bit1, bit2 = bits[half]
-        row, n, src, dst, to = (
-            ((1 - bit1) * row2, row2, sent, got1b, 0),
-            (bit1 * row2 + (1 - bit2) * row4, row4, sent2, y_s, 1),
-            (bit1 * row2 + bit2 * row4, row4, y_s, y_s, 1),
-            (bit1 * row2, row2, y_s, y_s, 0),
-        )[step]
-        at = (pl.ds(many(row, 16), n), columns_of(c, half))
-        pltpu.make_async_remote_copy(
-            src_ref=src.at[at], dst_ref=dst.at[at], send_sem=a2_send.at[step], recv_sem=chunk_recv(c, step),
-            device_id={"tp": plan[half][to]}, device_id_type=MESH,
-        ).start()
+    row2 = rows // 2
+
+    def halved_send(c, step):
+        for half in range(2):
+            row = (1 - kept[half]) * row2 if step == 0 else kept[half] * row2
+            at = (pl.ds(many(row, 32), row2), columns_of(c, half))
+            pltpu.make_async_remote_copy(
+                src_ref=(sent, sent2, y_s)[step].at[at], dst_ref=(got1b, y_s, y_s)[step].at[at], send_sem=a2_send.at[step],
+                recv_sem=a2_back.at[c] if step == 2 else a2_recv.at[c, step],
+                device_id={"tp": plan[half][step % 2]}, device_id_type=MESH,
+            ).start()
 
     @jax.named_scope("halved_step")
     def halved_step(c, step):
-        arrived((row2, row4, row4, row2)[step] * CHUNK, chunk_recv(c, step))
+        arrived(row2 * CHUNK, a2_back.at[c] if step == 2 else a2_recv.at[c, step])
+        if step == 2:
+            return
         for half in range(2):
-            bit1, bit2 = bits[half]
-            cols = columns_of(c, half)
+            at = (pl.ds(many(kept[half] * row2, 32), row2), columns_of(c, half))
             if step == 0:
-                at = (pl.ds(many(bit1 * row2 + (1 - bit2) * row4, 16), row4), cols)
                 sent2[at] = (part[at] + got1b[at].astype(F32)).astype(BF16)
-            elif step == 1:
-                at = (pl.ds(many(bit1 * row2 + bit2 * row4, 16), row4), cols)
-                y_s[at] = (
-                    x_s[at].astype(F32) + (part[at] + got1b[at].astype(F32) + y_s[at].astype(F32))
-                ).astype(BF16)
-            if step < 3:
-                halved_send(c, step + 1, half)
+            else:
+                y_s[at] = (x_s[at].astype(F32) + (sent2[at].astype(F32) + y_s[at].astype(F32))).astype(BF16)
+        halved_send(c, step + 1)
 
     def down(i):
         wait(chunk_copy(i), "chunk_wait")
@@ -418,7 +443,7 @@
         return jnp.dot(got1[:, :ff], pool[pl.ds(row, ff), pl.ds(lane, CHUNK)], preferred_element_type=F32)
 
     def down_body(i, _):
-        for step in (3, 2, 1, 0):
+        for step in (2, 1, 0):
             at = (step + 1) * LAG
 
             @pl.when((i >= at) & (i < HALVED + at))
@@ -433,12 +458,11 @@
 
         @pl.when(i < HALVED)
         def _():
-            cols = pl.ds(many(i * CHUNK, CHUNK), CHUNK)
-            part[:, cols] = down(i)
+            part[:, pl.ds(many(i * CHUNK, CHUNK), CHUNK)] = down(i)
             for half in range(2):
-                at = (pl.ds(many((1 - bits[half][0]) * row2, 16), row2), columns_of(i, half))
+                at = (pl.ds(many((1 - kept[half]) * row2, 32), row2), columns_of(i, half))
                 sent[at] = part[at].astype(BF16)
-                halved_send(i, 0, half)
+            halved_send(i, 0)
 
         @pl.when((i >= HALVED) & (i < chunks))
         def _():
@@ -447,9 +471,9 @@
 
         return 0
 
-    lax.fori_loop(0, max(chunks + 2 * LAG, HALVED + 4 * LAG), down_body, 0)
+    lax.fori_loop(0, max(chunks + 2 * LAG, HALVED + 3 * LAG), down_body, 0)
     whole = chunks - HALVED
-    for step, n in enumerate((HALVED * row2 + whole * rows, HALVED * row4 + whole * rows, HALVED * row4, HALVED * row2)):
+    for step, n in enumerate((HALVED * row2 + whole * rows, HALVED * row2 + whole * rows, HALVED * row2)):
         arrived(n * CHUNK, a2_send.at[step])
 
 
@@ -489,17 +513,14 @@
                 pltpu.VMEM((rows, d), BF16),
                 pltpu.VMEM((rows, d), BF16),
                 dma((4,)),
-                dma((d // UNIT,)),
-                dma((RING,)),
-                dma((1,)),
-                dma((UNITS * UNIT // (4 * SLAB),)),
                 dma((chunks,)),
+                dma((RING, 2)),
                 dma((2,)),
                 dma((2, len(GROUPS) - 1)),
                 dma((2, d // BLOCK)),
-                dma((4,)),
+                dma((3,)),
                 dma((chunks, 2)),
-                dma((HALVED, 2)),
+                dma((HALVED,)),
             ],
             compiler_params=pltpu.CompilerParams(
                 collective_id=0, has_side_effects=True, vmem_limit_bytes=66350000

time: 108 us -> 103 us (0.954)
  Pallas kernels: 107 us -> 102 us
    pallas_call x1, Pallas kernels: 107 us -> 102 us  [step(): pl.pallas_call(functools.partial(kernel, dims), out_shape=pltpu.VMEM((row...]
where the time goes in v3:
time: 103 us
  Pallas kernels  102 us (99%)
    pallas_call x1, Pallas kernels, step(): pl.pallas_call(functools.partial(kernel, dims), out_shape=pltpu.VMEM((row...  102 us

profile of v3, /device:TPU:112, one launch (start us, length us, event | category | flops | bytes accessed | tf_op | source)
XLA Modules:
  0.0 103.1 jit_solution(2599140730043765518)
XLA Ops:
  0.0 102.3 %shard_map.109 = bf16[64,5120]{1,0:T(8,128)(2,1)S(1)} custom-call(bf16[64,5120]{1,0:T(8,128)(2,1)} %x_hbm.1, bf16[20480,2048]{1,0:T(8,128)(2,1)} %bitcast.1.k_hbm, bf16[20480,2048]{1,0:T(8,128)(2,1)} %bitcast.3.v_hbm, bf16[40,128]{1,0:T(8,128)(2,1)} %bitcast.8, bf16[5120,1280]{1,0:T(8,128)(2,1)} %wq_hbm.1, bf16[1280,5120]{1,0:T(8,128)(2,1)} %wo_hbm.1, ...), custom_call_target="tpu_custom_call" | custom-call | tf_op jit(solution)/shard_map/pallas_call | solution.py:494
  102.3 0.8 copy.13

commit v4 on v3

--- a/solution.py
+++ b/solution.py
@@ -266,7 +266,7 @@
             scores = jnp.dot(q, pool[pl.ds(at + j * kvd, kvd), :WIDE], preferred_element_type=F32) * HEAD**-0.5
             top = jnp.max(scores, -1, keepdims=True)
             e = jnp.exp(scores - top)
-            ws.append(e / jnp.sum(e, -1, keepdims=True))
+            ws.append(e * (1 / jnp.sum(e, -1, keepdims=True)))
         w = jnp.concatenate(ws, 0).astype(BF16)
         if early:
             kv_wait(1, "v_wait")
@@ -281,7 +281,7 @@
         def _():
             start(kv_copies(i + RING))
 
-        @pl.when(i == 6)
+        @pl.when(i == 8)
         def _():
             start(wo_copies())
 
@@ -305,7 +305,8 @@
         return 0
 
     lax.fori_loop(0, GROUPS[0][1], lambda i, _: attend(i, True), 0)
-    lax.fori_loop(GROUPS[0][1], batches, lambda i, _: attend(i, False), 0)
+    lax.fori_loop(GROUPS[0][1], batches - 1, lambda i, _: attend(i, False), 0)
+    lax.fori_loop(batches - 1, batches, lambda i, _: attend(i, True), 0)
 
     gather_seen(exposed)
     blocks = d // BLOCK

time: 103 us -> 102 us (level)
  no operation moved by 1% of the time
where the time goes in v4:
time: 102 us
  Pallas kernels  102 us (100%)
    pallas_call x1, Pallas kernels, step(): pl.pallas_call(functools.partial(kernel, dims), out_shape=pltpu.VMEM((row...  102 us

profile of v4, /device:TPU:112, one launch (start us, length us, event | category | flops | bytes accessed | tf_op | source)
XLA Modules:
  0.0 102.4 jit_solution(4920224888763625160)
XLA Ops:
  0.0 101.5 %shard_map.109 = bf16[64,5120]{1,0:T(8,128)(2,1)S(1)} custom-call(bf16[64,5120]{1,0:T(8,128)(2,1)} %x_hbm.1, bf16[20480,2048]{1,0:T(8,128)(2,1)} %bitcast.1.k_hbm, bf16[20480,2048]{1,0:T(8,128)(2,1)} %bitcast.3.v_hbm, bf16[40,128]{1,0:T(8,128)(2,1)} %bitcast.8, bf16[5120,1280]{1,0:T(8,128)(2,1)} %wq_hbm.1, bf16[1280,5120]{1,0:T(8,128)(2,1)} %wo_hbm.1, ...), custom_call_target="tpu_custom_call" | custom-call | tf_op jit(solution)/shard_map/pallas_call | solution.py:495
  101.5 0.8 copy.13
